TPU v7x, 128 devices: a whole 4x4x4 slice. The times are simulated.
128 devices in a mesh: seg: 32 (over y_lo, x, z), rep: 4 (over y_hi, core).
Axes of the slice: x: 4, y: 4 (y_hi: 2, y_lo: 2; y = y_hi * 2 + y_lo), z: 4, core: 2. Of those that a mesh axis runs over, the one named last changes fastest.
Arguments:
- decoder_rows: bfloat16 [256, 4096], P('rep', 'seg'), may hold values from -2000 to 2000
- norm_gain: float32 [4096], replicated, may hold values from 0.5 to 1.5
- query_weight: bfloat16 [4096, 4096], P('rep', 'seg'), may hold values from -1 to 1
- key_codes: bfloat16 [4, 16384, 4096], P('rep', 'seg'), may hold values from -127 to 127, as said below
- key_scale: float32 [4, 128, 64], P('rep', 'seg'), may hold values from 0.5 to 1.5
- value_codes: bfloat16 [4, 16384, 4096], P('rep', 'seg'), may hold values from -6 to 6
- value_scale: float32 [4, 128, 64], P('rep', 'seg'), may hold values from 0.5 to 2
- enc_lengths: int32 [4], P('rep'), may hold values from 4096 to 16384
- output_weight: bfloat16 [4096, 4096], P('seg', 'rep'), may hold values from -0.09375 to 0.09375
Outputs:
- update: bfloat16 [256, 4096], P('rep', 'seg')
Inputs may be any that keep to these rules, and one draw needn't show every extreme that they name: `key_codes`: codes of a block times its scale give the cached keys.
All inputs are finite; a program needn't handle non-finite values.
Results may differ from a plain program's by a relative error of at most 0.011.
Values may be sent and summed in bfloat16 or wider, within the bound.
No kernel may reach another device: no remote copies, remote signals or barrier semaphores. Data moves between devices by JAX's collectives and lax.ppermute only.
A program may use at most 64 MiB of HBM per device.

v0:
```python
import jax
import jax.numpy as jnp
from jax import lax
from jax.sharding import PartitionSpec as P


def laid_out(tiles, dim):
    tiles = jnp.moveaxis(tiles, 0, dim)
    dims = tiles.shape
    return tiles.reshape(*dims[:dim], dims[dim] * dims[dim + 1], *dims[dim + 2 :])


def from_everyone(shard, axis):
    count = lax.axis_size(axis)
    return lax.all_to_all(
        jnp.broadcast_to(shard[None], (count, *shard.shape)), axis, 0, 0, tiled=True
    )


def gathered_copies(shard, axis, dim):
    return laid_out(from_everyone(shard, axis), dim)


def side_by_side(arrays, axis, split_dim, concat_dim, along):
    ends, at = ([], 0)
    for a in arrays[:-1]:
        at += a.shape[along]
        ends.append(at)
    both = jnp.concatenate(arrays, axis=along)
    return tuple(
        jnp.split(
            lax.all_to_all(both, axis, split_axis=split_dim, concat_axis=concat_dim, tiled=True),
            ends,
            axis=along,
        )
    )


def in_blocks(shard, dim, count):
    before, after = (shard.shape[:dim], shard.shape[dim + 1 :])
    return jnp.moveaxis(shard.reshape(*before, count, -1, *after), dim, 0)


def sent_and_summed(shard, axis, dim):
    tiles = in_blocks(shard, dim, lax.axis_size(axis))
    arrived = lax.all_to_all(tiles, axis, split_axis=0, concat_axis=0, tiled=True)
    return arrived.sum(axis=0)


def per_device(
    decoder_rows,
    norm_gain,
    query_weight,
    key_codes,
    key_scale,
    value_codes,
    value_scale,
    enc_lengths,
    output_weight,
):
    gathered = gathered_copies(decoder_rows, "seg", 1)
    widened = gathered.astype(jnp.float32)
    variance = jnp.mean(widened * widened, axis=-1, keepdims=True)
    normed = (widened * lax.rsqrt(variance + 1e-06) * norm_gain[None, :]).astype(jnp.bfloat16)
    query_own = jnp.dot(
        normed, gathered_copies(query_weight, "rep", 0), preferred_element_type=jnp.float32
    ).astype(jnp.bfloat16)
    queries = gathered_copies(query_own, "seg", 1)
    docs_here, seg_length, inner_width = key_codes.shape
    head_count = key_scale.shape[2]
    head_dim = inner_width // head_count
    block_length = seg_length // key_scale.shape[1]
    per_doc = queries.shape[0] // docs_here
    row_count = docs_here * per_doc
    first_pos = lax.axis_index("seg") * seg_length
    positions = first_pos + jnp.arange(seg_length, dtype=jnp.int32)

    def one_doc(group_members):
        (
            document_query,
            document_keys,
            document_values,
            document_key_scale,
            document_value_scale,
            document_length,
        ) = group_members
        split_query = document_query.reshape(per_doc, head_count, head_dim)
        split_keys = document_keys.reshape(seg_length, head_count, head_dim)
        split_values = document_values.reshape(seg_length, head_count, head_dim)
        attention_scores = jnp.einsum(
            "qhd,khd->qhk", split_query, split_keys, preferred_element_type=jnp.float32
        )
        key_multiplier = jnp.repeat(document_key_scale, block_length, axis=0).T
        value_factor = jnp.repeat(document_value_scale, block_length, axis=0).T
        attention_scores = attention_scores * key_multiplier[None]
        usable = (positions < document_length)[None, None, :]
        attention_scores = jnp.where(usable, attention_scores, jnp.float32(-1e30))
        peaks = jnp.max(attention_scores, axis=-1)
        weights = jnp.where(usable, jnp.exp(attention_scores - peaks[..., None]), jnp.float32(0.0))
        totals = jnp.sum(weights, axis=-1)
        scaled = (weights * value_factor[None]).astype(jnp.bfloat16)
        attended = jnp.einsum(
            "qhk,khd->qhd", scaled, split_values, preferred_element_type=jnp.float32
        )
        return (peaks, totals, attended.reshape(per_doc, inner_width))

    query_docs = queries.reshape(docs_here, per_doc, inner_width)
    peaks, totals, outputs = lax.map(
        one_doc, (query_docs, key_codes, value_codes, key_scale, value_scale, enc_lengths)
    )
    peaks = peaks.reshape(row_count, head_count)
    totals = totals.reshape(row_count, head_count)
    outputs = outputs.reshape(row_count, inner_width)
    seg_count = lax.axis_size("seg")
    own_heads = head_count // seg_count
    received = (
        *side_by_side((peaks[None], totals[None]), "seg", 2, 0, 1),
        lax.all_to_all(outputs[None], "seg", split_axis=2, concat_axis=0, tiled=True),
    )
    peak_all, total_all, out_all = received
    largest = jnp.max(peak_all, axis=0)
    factor = jnp.exp(peak_all - largest[None])
    denominator = jnp.sum(factor * total_all, axis=0)
    numerator = jnp.sum(
        out_all.reshape(seg_count, row_count, own_heads, head_dim) * factor[..., None], axis=0
    )
    attn_own = (
        (numerator / denominator[..., None])
        .reshape(row_count, own_heads * head_dim)
        .astype(jnp.bfloat16)
    )
    partial_terms = jnp.dot(
        attn_own, gathered_copies(output_weight, "rep", 1), preferred_element_type=jnp.float32
    )
    return sent_and_summed(partial_terms, "seg", 1).astype(jnp.bfloat16)


def solution(mesh):
    placed = (
        P("rep", "seg"),
        P(),
        P("rep", "seg"),
        P("rep", "seg", None),
        P("rep", "seg", None),
        P("rep", "seg", None),
        P("rep", "seg", None),
        P("rep"),
        P("seg", "rep"),
    )
    return jax.shard_map(
        per_device, mesh=mesh, in_specs=placed, out_specs=P("rep", "seg"), check_vma=False
    )
```

profile of v0, /device:TPU:0, one launch (start us, length us, event | category | flops | bytes accessed | tf_op | source)
XLA Modules:
  0.0 186.5 jit_solution(13017367994925692182)
XLA Ops:
  0.0 0.0 copy-start.2
  0.0 0.0 copy-start.3
  0.0 0.9 broadcast_in_dim.84
  0.9 20.6 %all_to_all.58 = bf16[32,64,128]{2,1,0:T(8,128)(2,1)S(1)} all-to-all(bf16[32,64,128]{2,1,0:T(8,128)(2,1)S(1)} %broadcast_in_dim.84), channel_id=1, replica_groups=mesh['seg'=32,'rep'=4] {'seg'}, dimensions={0} | all-to-all | bytes 1048576 | tf_op jit(solution)/shard_map/all_to_all | solution.py:15
  21.5 2.1 %broadcast_in_dim.85 = bf16[4,1024,128]{2,1,0:T(8,128)(2,1)} broadcast(bf16[1024,128]{1,0:T(8,128)(2,1)} %param.11), dimensions={1,2} | broadcast | bytes 1310720 | tf_op jit(solution)/shard_map/broadcast_in_dim | solution.py:16
  23.5 4.2 %all-to-all-start.1 = ((bf16[4,1024,128]{2,1,0:T(8,128)(2,1)}), bf16[4,1024,128]{2,1,0:T(8,128)(2,1)S(1)}, u32[]{:S(2)}, u32[]{:S(2)}) async-start(bf16[4,1024,128]{2,1,0:T(8,128)(2,1)} %broadcast_in_dim.85), calls=%async_computation.1 | async-start | bytes 2097152 | tf_op jit(solution)/shard_map/all_to_all | solution.py:15
  27.7 0.2 fusion.13
  27.9 15.7 %all-to-all-done.1 = bf16[4,1024,128]{2,1,0:T(8,128)(2,1)S(1)} async-done(((bf16[4,1024,128]{2,1,0:T(8,128)(2,1)}), bf16[4,1024,128]{2,1,0:T(8,128)(2,1)S(1)}, u32[]{:S(2)}, u32[]{:S(2)}) %all-to-all-start.1) | async-done | bytes 1048608 | tf_op jit(solution)/shard_map/all_to_all | solution.py:15
  43.6 1.1 convolution_convert_fusion
  44.7 0.9 broadcast_in_dim.86
  45.6 4.2 %all-to-all-start.2 = ((bf16[32,64,128]{2,1,0:T(8,128)(2,1)}), bf16[32,64,128]{2,1,0:T(8,128)(2,1)S(1)}, u32[]{:S(2)}, u32[]{:S(2)}) async-start(bf16[32,64,128]{2,1,0:T(8,128)(2,1)} %broadcast_in_dim.86), calls=%async_computation.2 | async-start | bytes 1048576 | tf_op jit(solution)/shard_map/all_to_all | solution.py:15
  49.8 0.0 copy-done.2
  49.9 0.1 copy.42
  50.0 0.0 copy-done.3
  50.0 0.1 copy.44
  50.7 6.5 %copy.40 = bf16[1,512,4096]{1,2,0:T(8,128)(2,1)} copy(bf16[1,512,4096]{2,1,0:T(8,128)(2,1)} %param.12) | data formatting | bytes 8388608 | tf_op args[3]
  57.2 6.5 %copy.45 = bf16[1,512,4096]{1,2,0:T(8,128)(2,1)} copy(bf16[1,512,4096]{2,1,0:T(8,128)(2,1)} %param.14) | data formatting | bytes 8388608 | tf_op args[5]
  63.7 0.1 broadcast_in_dim.87
  63.8 0.1 broadcast_in_dim.90
  64.0 0.0 all-to-all-done.2
  64.0 0.3 copy.39
  64.4 0.4 reshape.91
  64.8 4.2 %bitcast_reduce_fusion = (f32[64,64]{0,1:T(8,128)S(1)}, f32[64,64,512]{2,1,0:T(8,128)S(1)}) fusion(f32[64,512]{1,0:T(8,128)S(1)} %get-tuple-element.30, pred[512]{0:T(512)(128)(4,1)S(1)} %add_compare_fusion, bf16[512,64,64]{0,2,1:T(8,128)(2,1)} %bitcast.83, bf16[64,64,64]{2,1,0:T(8,128)(2,1)S(1)} %reshape.91), kind=kOutput, calls=%fused_computation.1 | convolution fusion | flops 274722816 | bytes 13255168 | tf_op jit(solution)/shard_map/while/body/eval_jaxpr/qhd,khd->qhk/dot_general | solution.py:90
  68.9 0.0 copy-start
  69.0 3.2 %copy-done = f32[64,64,512]{2,1,0:T(8,128)} copy-done((f32[64,64,512]{2,1,0:T(8,128)}, f32[64,64,512]{2,1,0:T(8,128)S(1)}, u32[]{:S(2)}) %copy-start) | copy-done | bytes 8388632
  72.2 2.8 %fusion.2 = f32[64,64]{0,1:T(8,128)S(1)} fusion(f32[64,64,512]{2,1,0:T(8,128)S(1)} %get-tuple-element.28, f32[64,64]{0,1:T(8,128)S(1)} %get-tuple-element.27, f32[64,512]{1,0:T(8,128)S(1)} %get-tuple-element.30, pred[512]{0:T(512)(128)(4,1)S(1)} %add_compare_fusion), kind=kLoop, calls=%fused_computation.6 | loop fusion | flops 10481664 | bytes 8552960 | tf_op jit(solution)/shard_map/while/body/eval_jaxpr/reduce_sum | solution.py:100
  75.0 0.7 pad_maximum_fusion
  75.7 8.5 %all-to-all-start.4 = ((f32[1,128,64]{1,0,2:T(1,128)}), f32[1,128,64]{1,0,2:T(1,128)S(1)}, u32[]{:S(2)}, u32[]{:S(2)}) async-start(f32[1,128,64]{1,0,2:T(1,128)} %pad_maximum_fusion), calls=%async_computation.4 | async-start | bytes 65536 | tf_op jit(solution)/shard_map/all_to_all | solution.py:32
  84.2 8.5 %fusion.12 = f32[64,64,64]{2,0,1:T(8,128)} fusion(bf16[512,64,64]{0,2,1:T(8,128)(2,1)} %bitcast.86, f32[64,64,512]{2,1,0:T(8,128)} %copy-done, f32[64,512]{1,0:T(8,128)S(1)} %get-tuple-element.29, f32[64,64]{0,1:T(8,128)S(1)} %get-tuple-element.27, f32[64,512]{1,0:T(8,128)S(1)} %get-tuple-element.30, pred[512]{0:T(512)(128)(4,1)S(1)} %add_compare_fusion), kind=kOutput, calls=%fused_computation.17 | convolution fusion | flops 281018368 | bytes 13910528 | tf_op jit(solution)/shard_map/while/body/eval_jaxpr/qhk,khd->qhd/dot_general | solution.py:102
  92.8 0.0 copy-start.1
  92.8 2.0 %copy.50 = f32[64,64,64]{0,2,1:T(8,128)S(1)} copy(f32[64,64,64]{2,0,1:T(8,128)} %fusion.12) | data formatting | bytes 2097152 | tf_op jit(solution)/shard_map/while/body/jit(dynamic_update_index_in_dim)/broadcast_in_dim | solution.py:108
  94.7 0.5 broadcast.48
  95.2 19.4 %reduce.3 = f32[4096,64]{1,0:T(8,128)} reduce(f32[4096,1,64]{2,1,0:T(1,128)S(1)} %bitcast.84, f32[]{:T(128)} %broadcast.48), dimensions={1}, to_apply=%bitcast.73.reduce_sub_computation | reduce | bytes 2097156
  114.6 3.4 %reshape.98 = f32[32,1,8192]{2,1,0:T(1,128)} reshape(f32[4096,64]{1,0:T(8,128)} %reduce.3) | data formatting | bytes 2097152
  118.1 0.0 all-to-all-done.4
  118.1 8.1 %all-to-all-start.3 = ((f32[32,1,8192]{2,1,0:T(1,128)}), f32[32,1,8192]{2,1,0:T(1,128)S(1)}, u32[]{:S(2)}, u32[]{:S(2)}) async-start(f32[32,1,8192]{2,1,0:T(1,128)} %reshape.98), calls=%async_computation.3 | async-start | bytes 2097152 | tf_op jit(solution)/shard_map/all_to_all | solution.py:118
  126.2 0.0 copy-done.1
  126.2 0.2 copy.49
  126.4 15.4 %all-to-all-done.3 = f32[32,1,8192]{2,1,0:T(1,128)S(1)} async-done(((f32[32,1,8192]{2,1,0:T(1,128)}), f32[32,1,8192]{2,1,0:T(1,128)S(1)}, u32[]{:S(2)}, u32[]{:S(2)}) %all-to-all-start.3) | async-done | bytes 1048608 | tf_op jit(solution)/shard_map/all_to_all | solution.py:118
  141.8 1.2 broadcast_in_dim.94
  142.9 4.5 %all-to-all-start.5 = ((bf16[4,128,1024]{1,2,0:T(8,128)(2,1)}), bf16[4,128,1024]{1,2,0:T(8,128)(2,1)}, u32[]{:S(2)}, u32[]{:S(2)}) async-start(bf16[4,128,1024]{1,2,0:T(8,128)(2,1)} %broadcast_in_dim.94), calls=%async_computation.5 | async-start | bytes 2097152 | tf_op jit(solution)/shard_map/all_to_all | solution.py:15
  147.4 0.1 fusion.21
  147.6 3.2 %reduce.4 = f32[32,8192]{1,0:T(8,128)S(1)} reduce(f32[32,1,8192]{2,1,0:T(1,128)S(1)} %all-to-all-done.3, f32[]{:T(128)} %broadcast.48), dimensions={1}, to_apply=%all_to_all.42.reduce_sub_computation | reduce | bytes 2097156 | tf_op jit(solution)/shard_map/all_to_all | solution.py:118
  150.8 2.6 %reshape.99 = f32[4096,1,64]{2,1,0:T(1,128)S(1)} reshape(f32[32,8192]{1,0:T(8,128)S(1)} %reduce.4) | data formatting | bytes 2097152
  153.4 0.3 fusion.11
  153.7 9.5 %all-to-all-done.5 = bf16[4,128,1024]{1,2,0:T(8,128)(2,1)} async-done(((bf16[4,128,1024]{1,2,0:T(8,128)(2,1)}), bf16[4,128,1024]{1,2,0:T(8,128)(2,1)}, u32[]{:S(2)}, u32[]{:S(2)}) %all-to-all-start.5) | async-done | bytes 1048608 | tf_op jit(solution)/shard_map/all_to_all | solution.py:15
  163.2 1.7 convolution_bitcast_fusion
  164.9 20.9 %all_to_all.59 = f32[32,64,128]{2,1,0:T(8,128)S(1)} all-to-all(f32[32,64,128]{2,1,0:T(8,128)S(1)} %convolution_bitcast_fusion), channel_id=1, replica_groups=mesh['seg'=32,'rep'=4] {'seg'}, dimensions={0} | all-to-all | bytes 2097152 | tf_op jit(solution)/shard_map/all_to_all | solution.py:46
  185.8 0.7 reduce_sum.53
  (5 shorter events, 0.1 us)
Async XLA Ops:
  0.0 49.8 %copy-start.2 = (f32[1,4,64]{2,1,0:T(4,128)S(1)}, f32[1,4,64]{2,1,0:T(4,128)}, u32[]{:S(2)}) copy-start(f32[1,4,64]{2,1,0:T(4,128)} %param.13) | copy-start | bytes 3076
  0.0 50.0 %copy-start.3 = (f32[1,4,64]{2,1,0:T(4,128)S(1)}, f32[1,4,64]{2,1,0:T(4,128)}, u32[]{:S(2)}) copy-start(f32[1,4,64]{2,1,0:T(4,128)} %param.15) | copy-start | bytes 3076
  23.5 20.1 %all-to-all-start.1 = ((bf16[4,1024,128]{2,1,0:T(8,128)(2,1)}), bf16[4,1024,128]{2,1,0:T(8,128)(2,1)S(1)}, u32[]{:S(2)}, u32[]{:S(2)}) async-start(bf16[4,1024,128]{2,1,0:T(8,128)(2,1)} %broadcast_in_dim.85), calls=%async_computation.1 | async-start | bytes 2097152 | tf_op jit(solution)/shard_map/all_to_all | solution.py:15
  45.6 18.4 %all-to-all-start.2 = ((bf16[32,64,128]{2,1,0:T(8,128)(2,1)}), bf16[32,64,128]{2,1,0:T(8,128)(2,1)S(1)}, u32[]{:S(2)}, u32[]{:S(2)}) async-start(bf16[32,64,128]{2,1,0:T(8,128)(2,1)} %broadcast_in_dim.86), calls=%async_computation.2 | async-start | bytes 1048576 | tf_op jit(solution)/shard_map/all_to_all | solution.py:15
  68.9 3.2 %copy-start = (f32[64,64,512]{2,1,0:T(8,128)}, f32[64,64,512]{2,1,0:T(8,128)S(1)}, u32[]{:S(2)}) copy-start(f32[64,64,512]{2,1,0:T(8,128)S(1)} %get-tuple-element.28) | copy-start | bytes 25165828
  75.7 42.3 %all-to-all-start.4 = ((f32[1,128,64]{1,0,2:T(1,128)}), f32[1,128,64]{1,0,2:T(1,128)S(1)}, u32[]{:S(2)}, u32[]{:S(2)}) async-start(f32[1,128,64]{1,0,2:T(1,128)} %pad_maximum_fusion), calls=%async_computation.4 | async-start | bytes 65536 | tf_op jit(solution)/shard_map/all_to_all | solution.py:32
  92.8 33.5 %copy-start.1 = (bf16[128,1024]{1,0:T(8,128)(2,1)S(1)}, bf16[128,1024]{1,0:T(8,128)(2,1)}, u32[]{:S(2)}) copy-start(bf16[128,1024]{1,0:T(8,128)(2,1)} %param.17) | copy-start | bytes 786436
  118.1 23.7 %all-to-all-start.3 = ((f32[32,1,8192]{2,1,0:T(1,128)}), f32[32,1,8192]{2,1,0:T(1,128)S(1)}, u32[]{:S(2)}, u32[]{:S(2)}) async-start(f32[32,1,8192]{2,1,0:T(1,128)} %reshape.98), calls=%async_computation.3 | async-start | bytes 2097152 | tf_op jit(solution)/shard_map/all_to_all | solution.py:118
  142.9 20.2 %all-to-all-start.5 = ((bf16[4,128,1024]{1,2,0:T(8,128)(2,1)}), bf16[4,128,1024]{1,2,0:T(8,128)(2,1)}, u32[]{:S(2)}, u32[]{:S(2)}) async-start(bf16[4,128,1024]{1,2,0:T(8,128)(2,1)} %broadcast_in_dim.94), calls=%async_computation.5 | async-start | bytes 2097152 | tf_op jit(solution)/shard_map/all_to_all | solution.py:15
where the time goes:
time: 188 us; the launch traced here: 186 us
  blocking collectives  41.5 us (22%)
  waiting for transfers between devices  40.6 us (22%)
  local copies, waits for them, and re-layouts  31.1 us (17%)
  starting transfers between devices  29.5 us (16%)
  other arithmetic  27.5 us (15%)
  matrix products  15.5 us (8%)
    all_to_all x3, waiting for transfers between devices, from_everyone(): lax.all_to_all(jnp.broadcast_to(shard[None], (count, *shard.shape)), axis...  25.2 us
    unnamed x14, local copies, waits for them, and re-layouts  23 us
    all_to_all x1, blocking collectives, sent_and_summed(): lax.all_to_all(tiles, axis, split_axis=0, concat_axis=0, tiled=True)  20.9 us
    all_to_all x1, blocking collectives, from_everyone(): lax.all_to_all(jnp.broadcast_to(shard[None], (count, *shard.shape)), axis...  20.6 us
    unnamed x1, other arithmetic  19.4 us
    all_to_all x1, waiting for transfers between devices, per_device(): lax.all_to_all(outputs[None], 'seg', split_axis=2, concat_axis=0, tiled=T...  15.4 us
    all_to_all x3, starting transfers between devices, from_everyone(): lax.all_to_all(jnp.broadcast_to(shard[None], (count, *shard.shape)), axis...  12.8 us
    dot_general x1, matrix products, one_doc(): jnp.einsum('qhk,khd->qhd', scaled, split_values, preferred_element_type=j...  8.53 us
  transfers between devices with their start and end apart: 5, of which 3 were waited for; matrix products, arithmetic and copies ran while one was open for 29% of the time, Pallas kernels for 0%

commit v1 on v0

--- a/solution.py
+++ b/solution.py
@@ -115,7 +115,12 @@
     own_heads = head_count // seg_count
     received = (
         *side_by_side((peaks[None], totals[None]), "seg", 2, 0, 1),
-        lax.all_to_all(outputs[None], "seg", split_axis=2, concat_axis=0, tiled=True),
+        jnp.concatenate(
+            lax.all_to_all(
+                jnp.stack(jnp.split(outputs[None], lax.axis_size("seg"), axis=2)), "seg", 0, 0
+            ),
+            axis=0,
+        ),
     )
     peak_all, total_all, out_all = received
     largest = jnp.max(peak_all, axis=0)

time: 188 us -> 180 us (0.957)
  other arithmetic: 27.5 us -> 6.05 us
  local copies, waits for them, and re-layouts: 31.1 us -> 46.8 us
  waiting for transfers between devices: 40.6 us -> 48 us
  matrix products: 15.5 us -> 10.9 us
  starting transfers between devices: 29.5 us -> 25 us
    unnamed x1 -> x0, other arithmetic: 19.4 us -> none
    unnamed x14 -> x44, local copies, waits for them, and re-layouts: 23 us -> 32 us
    all_to_all x1, waiting for transfers between devices: 0.01 us -> 7.7 us  [side_by_side(): lax.all_to_all(both, axis, split_axis=split_dim, concat_axis=concat_dim,...]
    dot_general x1, matrix products: 8.53 us -> 3.81 us  [one_doc(): jnp.einsum('qhk,khd->qhd', scaled, split_values, preferred_element_type=j...]
    all_to_all x1, starting transfers between devices: 8.15 us -> 3.93 us  [per_device(): lax.all_to_all(jnp.stack(jnp.split(outputs[None], lax.axis_size('seg'), a...]
    mul x0 -> x2, local copies, waits for them, and re-layouts: none -> 3.59 us  [per_device(): out_all.reshape(seg_count, row_count, own_heads, head_dim)]
    all_to_all x1 -> x0, other arithmetic: 3.22 us -> none  [per_device(): lax.all_to_all(outputs[None], 'seg', split_axis=2, concat_axis=0, tiled=T...]
    transpose x0 -> x1, local copies, waits for them, and re-layouts: none -> 2.85 us  [one_doc(): jnp.einsum('qhk,khd->qhd', scaled, split_values, preferred_element_type=j...]
  transfers between devices with their start and end apart: 5 -> 5, of which waited for: 3 -> 4; matrix products, arithmetic and copies ran while one was open for 29% -> 11% of each run, Pallas kernels for 0% -> 0%
where the time goes in v1:
time: 180 us; the launch traced here: 179 us
  waiting for transfers between devices  48 us (27%)
  local copies, waits for them, and re-layouts  46.8 us (26%)
  blocking collectives  41.7 us (23%)
  starting transfers between devices  25 us (14%)
  matrix products  10.9 us (6%)
  other arithmetic  6.05 us (3%)
    unnamed x44, local copies, waits for them, and re-layouts  32 us
    all_to_all x3, waiting for transfers between devices, from_everyone(): lax.all_to_all(jnp.broadcast_to(shard[None], (count, *shard.shape)), axis...  25.6 us
    all_to_all x1, blocking collectives, sent_and_summed(): lax.all_to_all(tiles, axis, split_axis=0, concat_axis=0, tiled=True)  21.1 us
    all_to_all x1, blocking collectives, from_everyone(): lax.all_to_all(jnp.broadcast_to(shard[None], (count, *shard.shape)), axis...  20.6 us
    all_to_all x1, waiting for transfers between devices, per_device(): lax.all_to_all(jnp.stack(jnp.split(outputs[None], lax.axis_size('seg'), a...  14.7 us
    all_to_all x3, starting transfers between devices, from_everyone(): lax.all_to_all(jnp.broadcast_to(shard[None], (count, *shard.shape)), axis...  12.8 us
    all_to_all x1, starting transfers between devices, side_by_side(): lax.all_to_all(both, axis, split_axis=split_dim, concat_axis=concat_dim,...  8.33 us
    all_to_all x1, waiting for transfers between devices, side_by_side(): lax.all_to_all(both, axis, split_axis=split_dim, concat_axis=concat_dim,...  7.7 us
  transfers between devices with their start and end apart: 5, of which 4 were waited for; matrix products, arithmetic and copies ran while one was open for 11% of the time, Pallas kernels for 0%

profile of v1, /device:TPU:0, one launch (start us, length us, event | category | flops | bytes accessed | tf_op | source)
XLA Modules:
  0.0 179.3 jit_solution(12158617641739664484)
XLA Ops:
  0.0 0.9 broadcast_in_dim.84
  0.9 20.6 %all_to_all.48 = bf16[32,64,128]{2,1,0:T(8,128)(2,1)S(1)} all-to-all(bf16[32,64,128]{2,1,0:T(8,128)(2,1)S(1)} %broadcast_in_dim.84), channel_id=1, replica_groups=mesh['seg'=32,'rep'=4] {'seg'}, dimensions={0} | all-to-all | bytes 1048576 | tf_op jit(solution)/shard_map/all_to_all | solution.py:15
  21.5 2.1 %broadcast_in_dim.85 = bf16[4,1024,128]{2,1,0:T(8,128)(2,1)} broadcast(bf16[1024,128]{1,0:T(8,128)(2,1)} %param.11), dimensions={1,2} | broadcast | bytes 1310720 | tf_op jit(solution)/shard_map/broadcast_in_dim | solution.py:16
  23.5 4.2 %all-to-all-start.1 = ((bf16[4,1024,128]{2,1,0:T(8,128)(2,1)}), bf16[4,1024,128]{2,1,0:T(8,128)(2,1)S(1)}, u32[]{:S(2)}, u32[]{:S(2)}) async-start(bf16[4,1024,128]{2,1,0:T(8,128)(2,1)} %broadcast_in_dim.85), calls=%async_computation.1 | async-start | bytes 2097152 | tf_op jit(solution)/shard_map/all_to_all | solution.py:15
  27.9 15.7 %all-to-all-done.1 = bf16[4,1024,128]{2,1,0:T(8,128)(2,1)S(1)} async-done(((bf16[4,1024,128]{2,1,0:T(8,128)(2,1)}), bf16[4,1024,128]{2,1,0:T(8,128)(2,1)S(1)}, u32[]{:S(2)}, u32[]{:S(2)}) %all-to-all-start.1) | async-done | bytes 1048608 | tf_op jit(solution)/shard_map/all_to_all | solution.py:15
  43.6 1.1 convolution_convert_fusion
  44.7 1.0 broadcast_in_dim.86
  45.7 4.2 %all-to-all-start.2 = ((bf16[32,64,128]{2,1,0:T(8,128)(2,1)}), bf16[32,64,128]{2,1,0:T(8,128)(2,1)S(1)}, u32[]{:S(2)}, u32[]{:S(2)}) async-start(bf16[32,64,128]{2,1,0:T(8,128)(2,1)} %broadcast_in_dim.86), calls=%async_computation.2 | async-start | bytes 1048576 | tf_op jit(solution)/shard_map/all_to_all | solution.py:15
  50.8 6.6 %copy.28 = bf16[1,512,4096]{1,2,0:T(8,128)(2,1)} copy(bf16[1,512,4096]{2,1,0:T(8,128)(2,1)} %param.12) | data formatting | bytes 8388608 | tf_op args[3]
  57.3 6.5 %copy.33 = bf16[1,512,4096]{1,2,0:T(8,128)(2,1)} copy(bf16[1,512,4096]{2,1,0:T(8,128)(2,1)} %param.14) | data formatting | bytes 8388608 | tf_op args[5]
  64.1 0.3 copy.27
  64.4 0.4 reshape.89
  64.8 4.3 %bitcast_reduce_fusion = (f32[64,64]{0,1:T(8,128)S(1)}, f32[64,64,512]{2,1,0:T(8,128)S(1)}) fusion(f32[64,512]{1,0:T(8,128)S(1)} %get-tuple-element.30, pred[512]{0:T(512)(128)(4,1)S(1)} %add_compare_fusion, bf16[512,64,64]{0,2,1:T(8,128)(2,1)} %bitcast.196, bf16[64,64,64]{2,1,0:T(8,128)(2,1)S(1)} %reshape.89), kind=kOutput, calls=%fused_computation.1 | convolution fusion | flops 274722816 | bytes 13255168 | tf_op jit(solution)/shard_map/while/body/eval_jaxpr/qhd,khd->qhk/dot_general | solution.py:90
  69.2 2.8 %fusion.2 = f32[64,64]{0,1:T(8,128)S(1)} fusion(f32[64,64,512]{2,1,0:T(8,128)S(1)} %get-tuple-element.28, f32[64,64]{0,1:T(8,128)S(1)} %get-tuple-element.27, f32[64,512]{1,0:T(8,128)S(1)} %get-tuple-element.30, pred[512]{0:T(512)(128)(4,1)S(1)} %add_compare_fusion), kind=kLoop, calls=%fused_computation.6 | loop fusion | flops 10481664 | bytes 8552960 | tf_op jit(solution)/shard_map/while/body/eval_jaxpr/reduce_sum | solution.py:100
  72.0 3.8 %fusion.11 = f32[64,64,64]{2,0,1:T(8,128)} fusion(bf16[512,64,64]{0,2,1:T(8,128)(2,1)S(1)} %bitcast.197, f32[64,64,512]{2,1,0:T(8,128)S(1)} %get-tuple-element.28, f32[64,512]{1,0:T(8,128)S(1)} %get-tuple-element.29, f32[64,64]{0,1:T(8,128)S(1)} %get-tuple-element.27, f32[64,512]{1,0:T(8,128)S(1)} %get-tuple-element.30, pred[512]{0:T(512)(128)(4,1)S(1)} %add_compare_fusion), kind=kOutput, calls=%fused_computation.15 | convolution fusion | flops 281018368 | bytes 13910528 | tf_op jit(solution)/shard_map/while/body/eval_jaxpr/qhk,khd->qhd/dot_general | solution.py:102
  75.8 2.9 %copy.34 = f32[64,64,64]{2,1,0:T(8,128)S(1)} copy(f32[64,64,64]{2,0,1:T(8,128)} %fusion.11) | data formatting | bytes 2097152 | tf_op jit(solution)/shard_map/while/body/eval_jaxpr/qhk,khd->qhd/transpose | solution.py:102
  78.6 0.7 broadcast_in_dim.91
  79.3 0.6 constant_dynamic-update-slice_fusion.31
  79.9 0.6 constant_dynamic-update-slice_fusion.30
  80.5 0.6 constant_dynamic-update-slice_fusion.29
  81.1 0.6 constant_dynamic-update-slice_fusion.28
  81.7 0.6 constant_dynamic-update-slice_fusion.27
  82.3 0.6 constant_dynamic-update-slice_fusion.26
  82.9 0.6 constant_dynamic-update-slice_fusion.25
  83.5 0.6 constant_dynamic-update-slice_fusion.24
  84.2 0.6 constant_dynamic-update-slice_fusion.23
  84.8 0.6 constant_dynamic-update-slice_fusion.22
  85.4 0.6 constant_dynamic-update-slice_fusion.21
  86.0 0.6 constant_dynamic-update-slice_fusion.20
  86.6 0.6 constant_dynamic-update-slice_fusion.19
  87.2 0.6 constant_dynamic-update-slice_fusion.18
  87.8 0.6 constant_dynamic-update-slice_fusion.17
  88.4 0.6 constant_dynamic-update-slice_fusion.16
  89.0 0.6 constant_dynamic-update-slice_fusion.15
  89.6 0.6 constant_dynamic-update-slice_fusion.14
  90.2 0.6 constant_dynamic-update-slice_fusion.13
  90.8 0.6 constant_dynamic-update-slice_fusion.12
  91.5 0.6 constant_dynamic-update-slice_fusion.11
  92.1 0.6 constant_dynamic-update-slice_fusion.10
  92.7 0.6 constant_dynamic-update-slice_fusion.9
  93.3 0.6 constant_dynamic-update-slice_fusion.8
  93.9 0.6 constant_dynamic-update-slice_fusion.7
  94.5 0.6 constant_dynamic-update-slice_fusion.6
  95.1 0.6 constant_dynamic-update-slice_fusion.5
  95.7 0.6 constant_dynamic-update-slice_fusion.4
  96.3 0.6 constant_dynamic-update-slice_fusion.3
  96.9 0.6 constant_dynamic-update-slice_fusion.2
  97.5 0.6 constant_dynamic-update-slice_fusion.1
  98.1 0.7 pad_maximum_fusion
  98.9 8.3 %all-to-all-start.4 = ((f32[1,128,64]{1,0,2:T(1,128)}), f32[1,128,64]{1,0,2:T(1,128)S(1)}, u32[]{:S(2)}, u32[]{:S(2)}) async-start(f32[1,128,64]{1,0,2:T(1,128)} %pad_maximum_fusion), calls=%async_computation.4 | async-start | bytes 65536 | tf_op jit(solution)/shard_map/all_to_all | solution.py:32
  107.2 0.6 constant_dynamic-update-slice_fusion
  107.8 7.7 %all-to-all-done.4 = f32[1,128,64]{1,0,2:T(1,128)S(1)} async-done(((f32[1,128,64]{1,0,2:T(1,128)}), f32[1,128,64]{1,0,2:T(1,128)S(1)}, u32[]{:S(2)}, u32[]{:S(2)}) %all-to-all-start.4) | async-done | bytes 32800 | tf_op jit(solution)/shard_map/all_to_all | solution.py:32
  115.5 3.9 %all-to-all-start.3 = ((f32[32,1,64,128]{3,2,1,0:T(8,128)}), f32[32,1,64,128]{3,2,1,0:T(8,128)S(1)}, u32[]{:S(2)}, u32[]{:S(2)}) async-start(f32[32,1,64,128]{3,2,1,0:T(8,128)} %constant_dynamic-update-slice_fusion), calls=%async_computation.3 | async-start | bytes 2097152 | tf_op jit(solution)/shard_map/all_to_all | solution.py:119
  119.6 14.7 %all-to-all-done.3 = f32[32,1,64,128]{3,2,1,0:T(8,128)S(1)} async-done(((f32[32,1,64,128]{3,2,1,0:T(8,128)}), f32[32,1,64,128]{3,2,1,0:T(8,128)S(1)}, u32[]{:S(2)}, u32[]{:S(2)}) %all-to-all-start.3) | async-done | bytes 1048608 | tf_op jit(solution)/shard_map/all_to_all | solution.py:119
  134.3 1.3 broadcast_in_dim.94
  135.6 4.4 %all-to-all-start.5 = ((bf16[4,128,1024]{1,2,0:T(8,128)(2,1)}), bf16[4,128,1024]{1,2,0:T(8,128)(2,1)}, u32[]{:S(2)}, u32[]{:S(2)}) async-start(bf16[4,128,1024]{1,2,0:T(8,128)(2,1)} %broadcast_in_dim.94), calls=%async_computation.5 | async-start | bytes 2097152 | tf_op jit(solution)/shard_map/all_to_all | solution.py:15
  140.2 0.4 copy.35
  140.6 2.5 %mul.80 = f32[32,64,2,64]{3,2,1,0:T(2,128)S(1)} broadcast(f32[32,64,2]{2,1,0:T(8,128)S(1)} %copy.35), dimensions={0,1,2} | broadcast | bytes 1064960 | tf_op jit(solution)/shard_map/mul | solution.py:130
  143.1 1.1 mul.81
  144.3 1.3 multiply_reduce_fusion
  146.0 9.9 %all-to-all-done.5 = bf16[4,128,1024]{1,2,0:T(8,128)(2,1)} async-done(((bf16[4,128,1024]{1,2,0:T(8,128)(2,1)}), bf16[4,128,1024]{1,2,0:T(8,128)(2,1)}, u32[]{:S(2)}, u32[]{:S(2)}) %all-to-all-start.5) | async-done | bytes 1048608 | tf_op jit(solution)/shard_map/all_to_all | solution.py:15
  155.8 1.7 convolution_bitcast_fusion
  157.5 21.1 %all_to_all.49 = f32[32,64,128]{2,1,0:T(8,128)S(1)} all-to-all(f32[32,64,128]{2,1,0:T(8,128)S(1)} %convolution_bitcast_fusion), channel_id=1, replica_groups=mesh['seg'=32,'rep'=4] {'seg'}, dimensions={0} | all-to-all | bytes 2097152 | tf_op jit(solution)/shard_map/all_to_all | solution.py:46
  178.6 0.7 reduce_sum.53
  (26 shorter events, 1.5 us)
Async XLA Ops:
  0.0 49.9 %copy-start.3 = (f32[1,4,64]{2,1,0:T(4,128)S(1)}, f32[1,4,64]{2,1,0:T(4,128)}, u32[]{:S(2)}) copy-start(f32[1,4,64]{2,1,0:T(4,128)} %param.13) | copy-start | bytes 3076
  0.0 50.0 %copy-start.4 = (f32[1,4,64]{2,1,0:T(4,128)S(1)}, f32[1,4,64]{2,1,0:T(4,128)}, u32[]{:S(2)}) copy-start(f32[1,4,64]{2,1,0:T(4,128)} %param.15) | copy-start | bytes 3076
  23.5 20.1 %all-to-all-start.1 = ((bf16[4,1024,128]{2,1,0:T(8,128)(2,1)}), bf16[4,1024,128]{2,1,0:T(8,128)(2,1)S(1)}, u32[]{:S(2)}, u32[]{:S(2)}) async-start(bf16[4,1024,128]{2,1,0:T(8,128)(2,1)} %broadcast_in_dim.85), calls=%async_computation.1 | async-start | bytes 2097152 | tf_op jit(solution)/shard_map/all_to_all | solution.py:15
  45.7 18.4 %all-to-all-start.2 = ((bf16[32,64,128]{2,1,0:T(8,128)(2,1)}), bf16[32,64,128]{2,1,0:T(8,128)(2,1)S(1)}, u32[]{:S(2)}, u32[]{:S(2)}) async-start(bf16[32,64,128]{2,1,0:T(8,128)(2,1)} %broadcast_in_dim.86), calls=%async_computation.2 | async-start | bytes 1048576 | tf_op jit(solution)/shard_map/all_to_all | solution.py:15
  64.8 7.1 %copy-start = (bf16[1,512,4096]{1,2,0:T(8,128)(2,1)S(1)}, bf16[1,512,4096]{1,2,0:T(8,128)(2,1)}, u32[]{:S(2)}) copy-start(bf16[1,512,4096]{1,2,0:T(8,128)(2,1)} %copy.33) | copy-start | bytes 12582916
  75.8 43.7 %copy-start.2 = (bf16[128,1024]{1,0:T(8,128)(2,1)S(1)}, bf16[128,1024]{1,0:T(8,128)(2,1)}, u32[]{:S(2)}) copy-start(bf16[128,1024]{1,0:T(8,128)(2,1)} %param.17) | copy-start | bytes 786436
  98.9 16.6 %all-to-all-start.4 = ((f32[1,128,64]{1,0,2:T(1,128)}), f32[1,128,64]{1,0,2:T(1,128)S(1)}, u32[]{:S(2)}, u32[]{:S(2)}) async-start(f32[1,128,64]{1,0,2:T(1,128)} %pad_maximum_fusion), calls=%async_computation.4 | async-start | bytes 65536 | tf_op jit(solution)/shard_map/all_to_all | solution.py:32
  115.5 18.8 %all-to-all-start.3 = ((f32[32,1,64,128]{3,2,1,0:T(8,128)}), f32[32,1,64,128]{3,2,1,0:T(8,128)S(1)}, u32[]{:S(2)}, u32[]{:S(2)}) async-start(f32[32,1,64,128]{3,2,1,0:T(8,128)} %constant_dynamic-update-slice_fusion), calls=%async_computation.3 | async-start | bytes 2097152 | tf_op jit(solution)/shard_map/all_to_all | solution.py:119
  134.3 5.8 %copy-start.1 = (f32[32,1,64,128]{3,2,1,0:T(8,128)}, f32[32,1,64,128]{3,2,1,0:T(8,128)S(1)}, u32[]{:S(2)}) copy-start(f32[32,1,64,128]{3,2,1,0:T(8,128)S(1)} %all-to-all-done.3) | copy-start | bytes 3145732
  135.6 20.2 %all-to-all-start.5 = ((bf16[4,128,1024]{1,2,0:T(8,128)(2,1)}), bf16[4,128,1024]{1,2,0:T(8,128)(2,1)}, u32[]{:S(2)}, u32[]{:S(2)}) async-start(bf16[4,128,1024]{1,2,0:T(8,128)(2,1)} %broadcast_in_dim.94), calls=%async_computation.5 | async-start | bytes 2097152 | tf_op jit(solution)/shard_map/all_to_all | solution.py:15
